TPU v7x, 32 devices: a whole 2x2x4 slice. The times are simulated.
32 devices in a mesh: gx: 4 (over z), gy: 2 (over x), gz: 4 (over y, core).
Axes of the slice: x: 2, y: 2, z: 4, core: 2. Of those that a mesh axis runs over, the one named last changes fastest.
Arguments:
- start_potential: float32 [64, 256, 512], P('gx', 'gy', 'gz'), may hold values from -0.9 to 2.1
- permittivity: float32 [64, 256, 512], P('gx', 'gy', 'gz'), may hold values from 1 to 8
- screening: float32 [64, 256, 512], P('gx', 'gy', 'gz'), may hold values from 0.05 to 2
- source: float32 [64, 256, 512], P('gx', 'gy', 'gz'), may hold values from -12 to 12
Outputs:
- potential: float32 [64, 256, 512], P('gx', 'gy', 'gz')
- residual_rms: float32 [3], replicated
- induced_charge: float32 [3], replicated
All inputs are finite; a program needn't handle non-finite values.
Results may differ from a plain program's by a relative error of at most 0.0003.
Values sent between devices are 32-bit elements; how exact they have to be, the bound alone decides.
No kernel may reach another device: no remote copies, remote signals or barrier semaphores. Data moves between devices by JAX's collectives and lax.ppermute only.
A program may use at most 64 MiB of HBM per device.

v0:
```python
import jax
import jax.numpy as jnp
from jax import lax
from jax.sharding import PartitionSpec as P

ITERS = 3


def padded_2(array, sides, width):
    for axis, dim in sides:
        size, length = (lax.axis_size(axis), array.shape[dim])
        up = [(i, (i + 1) % size) for i in range(size - 1)]
        down = [(j, i) for i, j in up]
        last = lax.slice_in_dim(array, length - width, length, axis=dim)
        initial = lax.slice_in_dim(array, 0, width, axis=dim)
        before = lax.ppermute(last, axis, up)
        after = lax.ppermute(initial, axis, down)
        array = jnp.concatenate([before, array, after], axis=dim)
    return array


def harmonic(left, right):
    total = left + right
    return 2.0 * left * right / jnp.where(total > 0, total, 1.0)


def neighbours(block):
    return [
        block[2:, 1:-1, 1:-1],
        block[:-2, 1:-1, 1:-1],
        block[1:-1, 2:, 1:-1],
        block[1:-1, :-2, 1:-1],
        block[1:-1, 1:-1, 2:],
        block[1:-1, 1:-1, :-2],
    ]


def relax(padded, weights_pad, screening, source):
    center = padded[1:-1, 1:-1, 1:-1]
    middle = weights_pad[1:-1, 1:-1, 1:-1]
    flux = jnp.zeros_like(center)
    diagonal = jnp.zeros_like(center)
    for near, other in zip(neighbours(padded), neighbours(weights_pad)):
        weight = harmonic(middle, other)
        flux = flux + weight * (center - near)
        diagonal = diagonal + weight
    induced = screening * jnp.sinh(center)
    residual = source - flux - induced
    diagonal = diagonal + screening * jnp.cosh(center)
    return (center, residual, jnp.where(diagonal > 0, diagonal, 1.0), induced)


def statistics(own_residual, own_induced, cells, charge_terms):
    squares = jnp.sum(own_residual * own_residual)
    square_sum, charge_sum = lax.psum((squares, jnp.sum(own_induced)), ("gx", "gy", "gz"))
    charge_terms.append(charge_sum / cells)
    return jnp.sqrt(square_sum / cells + 1e-06)


def body(start_potential, permittivity, screening, source):
    shape = start_potential.shape
    cells = (
        shape[0]
        * shape[1]
        * shape[2]
        * lax.axis_size("gx")
        * lax.axis_size("gy")
        * lax.axis_size("gz")
    )
    norms = []
    charge_terms = []
    weights_pad = padded_2(permittivity, (("gx", 0), ("gy", 1), ("gz", 2)), 1)
    potential = start_potential
    for iteration in range(ITERS):
        padded = padded_2(potential, (("gx", 0), ("gy", 1), ("gz", 2)), 1)
        center, residual, diagonal, induced = relax(padded, weights_pad, screening, source)
        rms = statistics(residual, induced, cells, charge_terms)
        norms.append(rms)
        potential = center + 1.0 / (1.0 + rms) * residual / diagonal
    charges = jnp.stack(charge_terms)
    return (potential, jnp.stack(norms), charges)


def solution(mesh):
    placed = (P("gx", "gy", "gz"), P("gx", "gy", "gz"), P("gx", "gy", "gz"), P("gx", "gy", "gz"))
    return jax.shard_map(
        body, mesh=mesh, in_specs=placed, out_specs=(P("gx", "gy", "gz"), P(), P()), check_vma=False
    )
```

profile of v0, /device:TPU:0, one launch (start us, length us, event | category | flops | bytes accessed | tf_op | source)
XLA Modules:
  0.0 297.7 jit_solution(15585116569991222834)
XLA Ops:
  0.6 0.9 fusion.102
  1.5 1.3 collective-permute-start
  2.8 5.6 %collective-permute-start.2 = (f32[1,128,128]{2,0,1:T(1,128)S(1)}, f32[1,128,128]{2,0,1:T(1,128)S(1)}, u32[]{:S(2)}, u32[]{:S(2)}) collective-permute-start(f32[1,128,128]{2,0,1:T(1,128)S(1)} %bitcast.12), channel_id=1, source_target_pairs={{0,8},{8,16},{16,24},{1,9},{9,17},{17,25},{2,10},{10,18},{18,26},{... | collective-permute-start | bytes 196616 | tf_op jit(solution)/shard_map/ppermute | solution.py:16
  8.4 0.9 fusion.103
  9.3 1.3 collective-permute-start.1
  10.6 4.7 %collective-permute-start.3 = (f32[1,128,128]{2,0,1:T(1,128)S(1)}, f32[1,128,128]{2,0,1:T(1,128)S(1)}, u32[]{:S(2)}, u32[]{:S(2)}) collective-permute-start(f32[1,128,128]{2,0,1:T(1,128)S(1)} %bitcast.10), channel_id=1, source_target_pairs={{0,8},{8,16},{16,24},{1,9},{9,17},{17,25},{2,10},{10,18},{18,26},{... | collective-permute-start | bytes 196616 | tf_op jit(solution)/shard_map/ppermute | solution.py:16
  15.3 4.7 %fusion.88 = (f32[]{:T(128)}, f32[16,128,128]{2,0,1:T(8,128)}, f32[16,128,128]{2,0,1:T(8,128)S(1)}) fusion(f32[16,128,128]{2,1,0:T(8,128)} %param.4, f32[16,128,128]{2,1,0:T(8,128)} %param.6), kind=kLoop, calls=%fused_computation.203 | loop fusion | flops 3145727 | bytes 4194308 | tf_op jit(solution)/shard_map/reduce_sum | solution.py:55
  20.1 0.6 copy.143
  20.7 1.3 collective-permute-start.4
  22.0 4.5 %collective-permute-start.6 = (f32[18,1,128]{2,0,1:T(8,128)S(1)}, f32[18,1,128]{2,0,1:T(8,128)S(1)}, u32[]{:S(2)}, u32[]{:S(2)}) collective-permute-start(f32[18,1,128]{2,0,1:T(8,128)S(1)} %get-tuple-element.44), channel_id=1, source_target_pairs={{0,4},{1,5},{2,6},{3,7},{8,12},{9,13},{10,14},{11,15},{16,20},{17,... | collective-permute-start | bytes 27656 | tf_op jit(solution)/shard_map/ppermute | solution.py:16
  26.6 1.3 collective-permute-start.7
  27.9 1.3 collective-permute-start.5
  29.5 2.1 fusion.98
  31.6 2.4 copy.168
  34.0 2.4 copy.162
  36.3 1.3 collective-permute-start.8
  37.6 3.0 %collective-permute-start.10 = (f32[18,130,1]{1,0,2:T(8,128)S(1)}, f32[18,130,1]{1,0,2:T(8,128)S(1)}, u32[]{:S(2)}, u32[]{:S(2)}) collective-permute-start(f32[18,130,1]{1,0,2:T(8,128)S(1)} %copy.168), channel_id=1, source_target_pairs={{0,1},{1,2},{2,3},{4,5},{5,6},{6,7},{8,9},{9,10},{10,11},{12,13},{... | collective-permute-start | bytes 28088 | tf_op jit(solution)/shard_map/ppermute | solution.py:16
  40.9 2.2 fusion.99
  43.1 2.4 copy.165
  45.5 1.3 collective-permute-start.9
  46.8 2.4 copy.171
  49.1 4.1 %collective-permute-start.11 = (f32[18,130,1]{1,0,2:T(8,128)S(1)}, f32[18,130,1]{1,0,2:T(8,128)S(1)}, u32[]{:S(2)}, u32[]{:S(2)}) collective-permute-start(f32[18,130,1]{1,0,2:T(8,128)S(1)} %copy.171), channel_id=1, source_target_pairs={{0,1},{1,2},{2,3},{4,5},{5,6},{6,7},{8,9},{9,10},{10,11},{12,13},{... | collective-permute-start | bytes 28088 | tf_op jit(solution)/shard_map/ppermute | solution.py:16
  53.3 2.1 copy.169
  55.4 2.1 copy.163
  57.5 2.1 copy.166
  59.6 2.1 copy.172
  61.7 9.7 %multiply_reduce_fusion.2 = (f32[]{:T(128)}, f32[16,128,128]{2,0,1:T(8,128)}, f32[16,128,128]{2,0,1:T(8,128)}, f32[16,128,128]{2,0,1:T(8,128)}) fusion(f32[16,128,128]{2,0,1:T(8,128)} %get-tuple-element.19, f32[16,128,128]{2,0,1:T(8,128)S(1)} %get-tuple-element.55, f32[18,1,128]{2,0,1:T(8,128)S(1)} %collective-permute-done.5, ...), kind=kLoop, calls=%fused_computation.183 | loop fusion | flops 23068672 | bytes 7676484 | tf_op jit(solution)/shard_map/reduce_sum | solution.py:54
  71.4 42.1 %psum.42 = f32[]{:T(128)} all-reduce(f32[]{:T(128)} %get-tuple-element.27), channel_id=1, replica_groups=mesh['gx'=4,'gy'=2,'gz'=4] {'gx','gy','gz'}, use_global_device_ids=true, to_apply=%region_1.2 | all-reduce | flops 1 | bytes 8 | tf_op jit(solution)/shard_map/psum | solution.py:55
  114.3 5.9 %fusion.16 = (f32[16,128,128]{2,0,1:T(8,128)S(1)}, f32[16,128,128]{2,0,1:T(8,128)}) fusion(f32[16,128,128]{2,0,1:T(8,128)} %get-tuple-element.28, f32[16,128,128]{2,1,0:T(8,128)S(1)} %copy-done, f32[]{:T(128)S(6)} %div.73, f32[16,128,128]{2,1,0:T(8,128)} %param.4, f32[16,128,128]{2,0,1:T(8,128)} %get-tuple-element.30, f32[16,128,128]{2,0,1:T(8,128)} %get-tuple-element.29, ...), kind=kLoop, calls=%fused_computation.32 | loop fusion | flops 11534336 | bytes 8538116 | tf_op jit(solution)/shard_map/add | solution.py:79
  120.3 2.2 collective-permute-start.13
  122.4 1.3 collective-permute-start.12
  123.7 0.6 collective-permute-done.13
  124.3 4.3 %collective-permute-done.12 = f32[1,128,128]{2,0,1:T(1,128)S(1)} collective-permute-done((f32[1,128,128]{2,0,1:T(1,128)S(1)}, f32[1,128,128]{2,0,1:T(1,128)S(1)}, u32[]{:S(2)}, u32[]{:S(2)}) %collective-permute-start.12) | collective-permute-done | bytes 65568 | tf_op jit(solution)/shard_map/ppermute | solution.py:17
  128.6 4.2 %collective-permute-start.15 = (f32[18,1,128]{2,0,1:T(8,128)S(1)}, f32[18,1,128]{2,0,1:T(8,128)S(1)}, u32[]{:S(2)}, u32[]{:S(2)}) collective-permute-start(f32[18,1,128]{2,0,1:T(8,128)S(1)} %get-tuple-element.41), channel_id=1, source_target_pairs={{0,4},{1,5},{2,6},{3,7},{8,12},{9,13},{10,14},{11,15},{16,20},{17,... | collective-permute-start | bytes 27656 | tf_op jit(solution)/shard_map/ppermute | solution.py:16
  132.8 1.3 collective-permute-start.14
  134.2 4.2 %collective-permute-done.14 = f32[18,1,128]{2,0,1:T(8,128)S(1)} collective-permute-done((f32[18,1,128]{2,0,1:T(8,128)S(1)}, f32[18,1,128]{2,0,1:T(8,128)S(1)}, u32[]{:S(2)}, u32[]{:S(2)}) %collective-permute-start.14) | collective-permute-done | bytes 9248 | tf_op jit(solution)/shard_map/ppermute | solution.py:17
  138.6 2.2 fusion.97
  140.8 2.4 copy.182
  143.2 1.3 collective-permute-start.16
  144.5 2.4 copy.184
  146.8 3.0 %collective-permute-start.17 = (f32[18,130,1]{1,0,2:T(8,128)S(1)}, f32[18,130,1]{1,0,2:T(8,128)S(1)}, u32[]{:S(2)}, u32[]{:S(2)}) collective-permute-start(f32[18,130,1]{1,0,2:T(8,128)S(1)} %copy.184), channel_id=1, source_target_pairs={{0,1},{1,2},{2,3},{4,5},{5,6},{6,7},{8,9},{9,10},{10,11},{12,13},{... | collective-permute-start | bytes 28088 | tf_op jit(solution)/shard_map/ppermute | solution.py:16
  149.9 2.1 copy.183
  152.0 2.1 copy.185
  154.1 8.9 %multiply_reduce_fusion.1 = (f32[]{:T(128)}, f32[16,128,128]{2,0,1:T(8,128)}) fusion(f32[16,128,128]{2,0,1:T(8,128)S(1)} %get-tuple-element.25, f32[16,128,128]{2,1,0:T(8,128)S(1)} %copy-done, f32[16,128,128]{2,0,1:T(8,128)} %get-tuple-element.30, f32[18,1,128]{2,0,1:T(8,128)S(1)} %collective-permute-done.14, ...), kind=kLoop, calls=%fused_computation.178 | loop fusion | flops 20709376 | bytes 7657764 | tf_op jit(solution)/shard_map/reduce_sum | solution.py:54
  163.0 39.6 %psum.43 = f32[]{:T(128)} all-reduce(f32[]{:T(128)} %get-tuple-element.23), channel_id=1, replica_groups=mesh['gx'=4,'gy'=2,'gz'=4] {'gx','gy','gz'}, use_global_device_ids=true, to_apply=%region_3.4 | all-reduce | flops 1 | bytes 8 | tf_op jit(solution)/shard_map/psum | solution.py:55
  203.3 4.5 %fusion.87 = (f32[]{:T(128)}, f32[]{:T(128)}, f32[16,128,128]{2,0,1:T(8,128)S(1)}) fusion(f32[16,128,128]{2,0,1:T(8,128)S(1)} %get-tuple-element.25, f32[16,128,128]{2,1,0:T(8,128)S(1)} %copy-done, f32[16,128,128]{2,0,1:T(8,128)} %get-tuple-element.26, f32[16,128,128]{2,0,1:T(8,128)} %get-tuple-element.24, f32[]{:T(128)S(6)} %div.76), kind=kLoop, calls=%fused_computation.202 | loop fusion | flops 8388606 | bytes 5242892 | tf_op jit(solution)/shard_map/reduce_sum | solution.py:55
  207.9 2.2 collective-permute-start.19
  210.1 1.3 collective-permute-start.18
  212.0 4.3 %collective-permute-done.18 = f32[1,128,128]{2,0,1:T(1,128)S(1)} collective-permute-done((f32[1,128,128]{2,0,1:T(1,128)S(1)}, f32[1,128,128]{2,0,1:T(1,128)S(1)}, u32[]{:S(2)}, u32[]{:S(2)}) %collective-permute-start.18) | collective-permute-done | bytes 65568 | tf_op jit(solution)/shard_map/ppermute | solution.py:17
  216.3 4.2 %collective-permute-start.21 = (f32[18,1,128]{2,0,1:T(8,128)S(1)}, f32[18,1,128]{2,0,1:T(8,128)S(1)}, u32[]{:S(2)}, u32[]{:S(2)}) collective-permute-start(f32[18,1,128]{2,0,1:T(8,128)S(1)} %get-tuple-element.39), channel_id=1, source_target_pairs={{0,4},{1,5},{2,6},{3,7},{8,12},{9,13},{10,14},{11,15},{16,20},{17,... | collective-permute-start | bytes 27656 | tf_op jit(solution)/shard_map/ppermute | solution.py:16
  220.5 1.5 collective-permute-start.20
  222.0 4.1 %collective-permute-done.20 = f32[18,1,128]{2,0,1:T(8,128)S(1)} collective-permute-done((f32[18,1,128]{2,0,1:T(8,128)S(1)}, f32[18,1,128]{2,0,1:T(8,128)S(1)}, u32[]{:S(2)}, u32[]{:S(2)}) %collective-permute-start.20) | collective-permute-done | bytes 9248 | tf_op jit(solution)/shard_map/ppermute | solution.py:17
  226.3 2.2 fusion.96
  228.5 2.4 copy.189
  230.8 1.3 collective-permute-start.22
  232.1 2.4 copy.191
  234.5 3.2 %collective-permute-start.23 = (f32[18,130,1]{1,0,2:T(8,128)S(1)}, f32[18,130,1]{1,0,2:T(8,128)S(1)}, u32[]{:S(2)}, u32[]{:S(2)}) collective-permute-start(f32[18,130,1]{1,0,2:T(8,128)S(1)} %copy.191), channel_id=1, source_target_pairs={{0,1},{1,2},{2,3},{4,5},{5,6},{6,7},{8,9},{9,10},{10,11},{12,13},{... | collective-permute-start | bytes 28088 | tf_op jit(solution)/shard_map/ppermute | solution.py:16
  237.7 2.1 copy.190
  239.8 2.1 copy.192
  241.9 8.9 %multiply_reduce_fusion = (f32[]{:T(128)}, f32[16,128,128]{2,0,1:T(8,128)}) fusion(f32[16,128,128]{2,0,1:T(8,128)S(1)} %copy-done.2, f32[16,128,128]{2,1,0:T(8,128)S(1)} %copy-done, f32[16,128,128]{2,0,1:T(8,128)} %get-tuple-element.30, f32[18,1,128]{2,0,1:T(8,128)S(1)} %collective-permute-done.20, f32[1,128,128]{2,0,1:T(1,128)S(1)} %collective-permute-done.18, ...), kind=kLoop, calls=%fused_computation.174 | loop fusion | flops 20709376 | bytes 7657764 | tf_op jit(solution)/shard_map/reduce_sum | solution.py:54
  250.8 39.9 %all-reduce = (f32[]{:T(128)}, f32[]{:T(128)}, f32[]{:T(128)}, f32[]{:T(128)}) all-reduce(f32[]{:T(128)} %get-tuple-element.21, f32[]{:T(128)} %get-tuple-element.13, f32[]{:T(128)} %get-tuple-element.12, f32[]{:T(128)} %get-tuple-element.18), channel_id=1, replica_groups=mesh['gx'=4,'gy'=2,'gz'=4] {'gx','gy','gz'}, use_global_device_ids=true, to_apply=%region_5.6 | all-reduce | flops 4 | bytes 32 | tf_op jit(solution)/shard_map/psum | solution.py:55
  293.3 2.5 fusion.20
  295.8 1.3 copy.196
  297.1 0.6 pad_maximum_fusion.88
  (37 shorter events, 1.9 us)
Async XLA Ops:
  1.5 19.1 %collective-permute-start = (f32[1,128,128]{2,0,1:T(1,128)S(1)}, f32[1,128,128]{2,0,1:T(1,128)S(1)}, u32[]{:S(2)}, u32[]{:S(2)}) collective-permute-start(f32[1,128,128]{2,0,1:T(1,128)S(1)} %bitcast.13), channel_id=1, source_target_pairs={{8,0},{16,8},{24,16},{9,1},{17,9},{25,17},{10,2},{18,10},{26,18},{... | collective-permute-start | bytes 196616 | tf_op jit(solution)/shard_map/ppermute | solution.py:17
  2.8 17.9 %collective-permute-start.2 = (f32[1,128,128]{2,0,1:T(1,128)S(1)}, f32[1,128,128]{2,0,1:T(1,128)S(1)}, u32[]{:S(2)}, u32[]{:S(2)}) collective-permute-start(f32[1,128,128]{2,0,1:T(1,128)S(1)} %bitcast.12), channel_id=1, source_target_pairs={{0,8},{8,16},{16,24},{1,9},{9,17},{17,25},{2,10},{10,18},{18,26},{... | collective-permute-start | bytes 196616 | tf_op jit(solution)/shard_map/ppermute | solution.py:16
  9.3 17.3 %collective-permute-start.1 = (f32[1,128,128]{2,0,1:T(1,128)S(1)}, f32[1,128,128]{2,0,1:T(1,128)S(1)}, u32[]{:S(2)}, u32[]{:S(2)}) collective-permute-start(f32[1,128,128]{2,0,1:T(1,128)S(1)} %bitcast.11), channel_id=1, source_target_pairs={{8,0},{16,8},{24,16},{9,1},{17,9},{25,17},{10,2},{18,10},{26,18},{... | collective-permute-start | bytes 196616 | tf_op jit(solution)/shard_map/ppermute | solution.py:17
  10.6 9.4 %copy-start.3 = (f32[16,128,128]{2,1,0:T(8,128)S(1)}, f32[16,128,128]{2,1,0:T(8,128)}, u32[]{:S(2)}) copy-start(f32[16,128,128]{2,1,0:T(8,128)} %param.5) | copy-start | bytes 3145732
  10.6 16.0 %collective-permute-start.3 = (f32[1,128,128]{2,0,1:T(1,128)S(1)}, f32[1,128,128]{2,0,1:T(1,128)S(1)}, u32[]{:S(2)}, u32[]{:S(2)}) collective-permute-start(f32[1,128,128]{2,0,1:T(1,128)S(1)} %bitcast.10), channel_id=1, source_target_pairs={{0,8},{8,16},{16,24},{1,9},{9,17},{17,25},{2,10},{10,18},{18,26},{... | collective-permute-start | bytes 196616 | tf_op jit(solution)/shard_map/ppermute | solution.py:16
  20.7 8.5 %collective-permute-start.4 = (f32[18,1,128]{2,0,1:T(8,128)S(1)}, f32[18,1,128]{2,0,1:T(8,128)S(1)}, u32[]{:S(2)}, u32[]{:S(2)}) collective-permute-start(f32[18,1,128]{2,0,1:T(8,128)S(1)} %get-tuple-element.43), channel_id=1, source_target_pairs={{4,0},{5,1},{6,2},{7,3},{12,8},{13,9},{14,10},{15,11},{20,16},{21,... | collective-permute-start | bytes 27656 | tf_op jit(solution)/shard_map/ppermute | solution.py:17
  22.0 7.2 %collective-permute-start.6 = (f32[18,1,128]{2,0,1:T(8,128)S(1)}, f32[18,1,128]{2,0,1:T(8,128)S(1)}, u32[]{:S(2)}, u32[]{:S(2)}) collective-permute-start(f32[18,1,128]{2,0,1:T(8,128)S(1)} %get-tuple-element.44), channel_id=1, source_target_pairs={{0,4},{1,5},{2,6},{3,7},{8,12},{9,13},{10,14},{11,15},{16,20},{17,... | collective-permute-start | bytes 27656 | tf_op jit(solution)/shard_map/ppermute | solution.py:16
  26.6 14.1 %collective-permute-start.7 = (f32[18,1,128]{2,0,1:T(8,128)S(1)}, f32[18,1,128]{2,0,1:T(8,128)S(1)}, u32[]{:S(2)}, u32[]{:S(2)}) collective-permute-start(f32[18,1,128]{2,0,1:T(8,128)S(1)} %get-tuple-element.45), channel_id=1, source_target_pairs={{0,4},{1,5},{2,6},{3,7},{8,12},{9,13},{10,14},{11,15},{16,20},{17,... | collective-permute-start | bytes 27656 | tf_op jit(solution)/shard_map/ppermute | solution.py:16
  27.9 12.8 %collective-permute-start.5 = (f32[18,1,128]{2,0,1:T(8,128)S(1)}, f32[18,1,128]{2,0,1:T(8,128)S(1)}, u32[]{:S(2)}, u32[]{:S(2)}) collective-permute-start(f32[18,1,128]{2,0,1:T(8,128)S(1)} %get-tuple-element.46), channel_id=1, source_target_pairs={{4,0},{5,1},{6,2},{7,3},{12,8},{13,9},{14,10},{15,11},{20,16},{21,... | collective-permute-start | bytes 27656 | tf_op jit(solution)/shard_map/ppermute | solution.py:17
  36.3 19.1 %collective-permute-start.8 = (f32[18,130,1]{1,0,2:T(8,128)S(1)}, f32[18,130,1]{1,0,2:T(8,128)S(1)}, u32[]{:S(2)}, u32[]{:S(2)}) collective-permute-start(f32[18,130,1]{1,0,2:T(8,128)S(1)} %copy.162), channel_id=1, source_target_pairs={{1,0},{2,1},{3,2},{5,4},{6,5},{7,6},{9,8},{10,9},{11,10},{13,12},{... | collective-permute-start | bytes 28088 | tf_op jit(solution)/shard_map/ppermute | solution.py:17
  37.6 15.6 %collective-permute-start.10 = (f32[18,130,1]{1,0,2:T(8,128)S(1)}, f32[18,130,1]{1,0,2:T(8,128)S(1)}, u32[]{:S(2)}, u32[]{:S(2)}) collective-permute-start(f32[18,130,1]{1,0,2:T(8,128)S(1)} %copy.168), channel_id=1, source_target_pairs={{0,1},{1,2},{2,3},{4,5},{5,6},{6,7},{8,9},{9,10},{10,11},{12,13},{... | collective-permute-start | bytes 28088 | tf_op jit(solution)/shard_map/ppermute | solution.py:16
  45.5 12.1 %collective-permute-start.9 = (f32[18,130,1]{1,0,2:T(8,128)S(1)}, f32[18,130,1]{1,0,2:T(8,128)S(1)}, u32[]{:S(2)}, u32[]{:S(2)}) collective-permute-start(f32[18,130,1]{1,0,2:T(8,128)S(1)} %copy.165), channel_id=1, source_target_pairs={{1,0},{2,1},{3,2},{5,4},{6,5},{7,6},{9,8},{10,9},{11,10},{13,12},{... | collective-permute-start | bytes 28088 | tf_op jit(solution)/shard_map/ppermute | solution.py:17
  49.1 10.5 %collective-permute-start.11 = (f32[18,130,1]{1,0,2:T(8,128)S(1)}, f32[18,130,1]{1,0,2:T(8,128)S(1)}, u32[]{:S(2)}, u32[]{:S(2)}) collective-permute-start(f32[18,130,1]{1,0,2:T(8,128)S(1)} %copy.171), channel_id=1, source_target_pairs={{0,1},{1,2},{2,3},{4,5},{5,6},{6,7},{8,9},{9,10},{10,11},{12,13},{... | collective-permute-start | bytes 28088 | tf_op jit(solution)/shard_map/ppermute | solution.py:16
  61.7 52.6 %copy-start = (f32[16,128,128]{2,1,0:T(8,128)S(1)}, f32[16,128,128]{2,1,0:T(8,128)}, u32[]{:S(2)}) copy-start(f32[16,128,128]{2,1,0:T(8,128)} %param.6) | copy-start | bytes 3145732
  120.3 4.0 %collective-permute-start.13 = (f32[1,128,128]{2,0,1:T(1,128)S(1)}, f32[1,128,128]{2,0,1:T(1,128)S(1)}, u32[]{:S(2)}, u32[]{:S(2)}) collective-permute-start(f32[1,128,128]{2,0,1:T(1,128)S(1)} %get-tuple-element.49), channel_id=1, source_target_pairs={{0,8},{8,16},{16,24},{1,9},{9,17},{17,25},{2,10},{10,18},{18,26},{... | collective-permute-start | bytes 196616 | tf_op jit(solution)/shard_map/ppermute | solution.py:16
  122.4 6.2 %collective-permute-start.12 = (f32[1,128,128]{2,0,1:T(1,128)S(1)}, f32[1,128,128]{2,0,1:T(1,128)S(1)}, u32[]{:S(2)}, u32[]{:S(2)}) collective-permute-start(f32[1,128,128]{2,0,1:T(1,128)S(1)} %get-tuple-element.50), channel_id=1, source_target_pairs={{8,0},{16,8},{24,16},{9,1},{17,9},{25,17},{10,2},{18,10},{26,18},{... | collective-permute-start | bytes 196616 | tf_op jit(solution)/shard_map/ppermute | solution.py:17
  128.6 5.6 %collective-permute-start.15 = (f32[18,1,128]{2,0,1:T(8,128)S(1)}, f32[18,1,128]{2,0,1:T(8,128)S(1)}, u32[]{:S(2)}, u32[]{:S(2)}) collective-permute-start(f32[18,1,128]{2,0,1:T(8,128)S(1)} %get-tuple-element.41), channel_id=1, source_target_pairs={{0,4},{1,5},{2,6},{3,7},{8,12},{9,13},{10,14},{11,15},{16,20},{17,... | collective-permute-start | bytes 27656 | tf_op jit(solution)/shard_map/ppermute | solution.py:16
  132.8 5.6 %collective-permute-start.14 = (f32[18,1,128]{2,0,1:T(8,128)S(1)}, f32[18,1,128]{2,0,1:T(8,128)S(1)}, u32[]{:S(2)}, u32[]{:S(2)}) collective-permute-start(f32[18,1,128]{2,0,1:T(8,128)S(1)} %get-tuple-element.42), channel_id=1, source_target_pairs={{4,0},{5,1},{6,2},{7,3},{12,8},{13,9},{14,10},{15,11},{20,16},{21,... | collective-permute-start | bytes 27656 | tf_op jit(solution)/shard_map/ppermute | solution.py:17
  143.2 6.7 %collective-permute-start.16 = (f32[18,130,1]{1,0,2:T(8,128)S(1)}, f32[18,130,1]{1,0,2:T(8,128)S(1)}, u32[]{:S(2)}, u32[]{:S(2)}) collective-permute-start(f32[18,130,1]{1,0,2:T(8,128)S(1)} %copy.182), channel_id=1, source_target_pairs={{1,0},{2,1},{3,2},{5,4},{6,5},{7,6},{9,8},{10,9},{11,10},{13,12},{... | collective-permute-start | bytes 28088 | tf_op jit(solution)/shard_map/ppermute | solution.py:17
  146.8 5.1 %collective-permute-start.17 = (f32[18,130,1]{1,0,2:T(8,128)S(1)}, f32[18,130,1]{1,0,2:T(8,128)S(1)}, u32[]{:S(2)}, u32[]{:S(2)}) collective-permute-start(f32[18,130,1]{1,0,2:T(8,128)S(1)} %copy.184), channel_id=1, source_target_pairs={{0,1},{1,2},{2,3},{4,5},{5,6},{6,7},{8,9},{9,10},{10,11},{12,13},{... | collective-permute-start | bytes 28088 | tf_op jit(solution)/shard_map/ppermute | solution.py:16
  207.8 18.3 %copy-start.1 = (f32[16,128,128]{2,0,1:T(8,128)}, f32[16,128,128]{2,0,1:T(8,128)S(1)}, u32[]{:S(2)}) copy-start(f32[16,128,128]{2,0,1:T(8,128)S(1)} %get-tuple-element.20) | copy-start | bytes 3145732
  207.9 4.1 %collective-permute-start.19 = (f32[1,128,128]{2,0,1:T(1,128)S(1)}, f32[1,128,128]{2,0,1:T(1,128)S(1)}, u32[]{:S(2)}, u32[]{:S(2)}) collective-permute-start(f32[1,128,128]{2,0,1:T(1,128)S(1)} %get-tuple-element.47), channel_id=1, source_target_pairs={{0,8},{8,16},{16,24},{1,9},{9,17},{17,25},{2,10},{10,18},{18,26},{... | collective-permute-start | bytes 196616 | tf_op jit(solution)/shard_map/ppermute | solution.py:16
  210.1 6.2 %collective-permute-start.18 = (f32[1,128,128]{2,0,1:T(1,128)S(1)}, f32[1,128,128]{2,0,1:T(1,128)S(1)}, u32[]{:S(2)}, u32[]{:S(2)}) collective-permute-start(f32[1,128,128]{2,0,1:T(1,128)S(1)} %get-tuple-element.48), channel_id=1, source_target_pairs={{8,0},{16,8},{24,16},{9,1},{17,9},{25,17},{10,2},{18,10},{26,18},{... | collective-permute-start | bytes 196616 | tf_op jit(solution)/shard_map/ppermute | solution.py:17
  216.3 5.7 %collective-permute-start.21 = (f32[18,1,128]{2,0,1:T(8,128)S(1)}, f32[18,1,128]{2,0,1:T(8,128)S(1)}, u32[]{:S(2)}, u32[]{:S(2)}) collective-permute-start(f32[18,1,128]{2,0,1:T(8,128)S(1)} %get-tuple-element.39), channel_id=1, source_target_pairs={{0,4},{1,5},{2,6},{3,7},{8,12},{9,13},{10,14},{11,15},{16,20},{17,... | collective-permute-start | bytes 27656 | tf_op jit(solution)/shard_map/ppermute | solution.py:16
  220.5 5.6 %collective-permute-start.20 = (f32[18,1,128]{2,0,1:T(8,128)S(1)}, f32[18,1,128]{2,0,1:T(8,128)S(1)}, u32[]{:S(2)}, u32[]{:S(2)}) collective-permute-start(f32[18,1,128]{2,0,1:T(8,128)S(1)} %get-tuple-element.40), channel_id=1, source_target_pairs={{4,0},{5,1},{6,2},{7,3},{12,8},{13,9},{14,10},{15,11},{20,16},{21,... | collective-permute-start | bytes 27656 | tf_op jit(solution)/shard_map/ppermute | solution.py:17
  230.8 6.8 %collective-permute-start.22 = (f32[18,130,1]{1,0,2:T(8,128)S(1)}, f32[18,130,1]{1,0,2:T(8,128)S(1)}, u32[]{:S(2)}, u32[]{:S(2)}) collective-permute-start(f32[18,130,1]{1,0,2:T(8,128)S(1)} %copy.189), channel_id=1, source_target_pairs={{1,0},{2,1},{3,2},{5,4},{6,5},{7,6},{9,8},{10,9},{11,10},{13,12},{... | collective-permute-start | bytes 28088 | tf_op jit(solution)/shard_map/ppermute | solution.py:17
  234.5 7.4 %copy-start.2 = (f32[16,128,128]{2,0,1:T(8,128)S(1)}, f32[16,128,128]{2,0,1:T(8,128)}, u32[]{:S(2)}) copy-start(f32[16,128,128]{2,0,1:T(8,128)} %copy-done.1) | copy-start | bytes 3145732
  234.5 5.3 %collective-permute-start.23 = (f32[18,130,1]{1,0,2:T(8,128)S(1)}, f32[18,130,1]{1,0,2:T(8,128)S(1)}, u32[]{:S(2)}, u32[]{:S(2)}) collective-permute-start(f32[18,130,1]{1,0,2:T(8,128)S(1)} %copy.191), channel_id=1, source_target_pairs={{0,1},{1,2},{2,3},{4,5},{5,6},{6,7},{8,9},{9,10},{10,11},{12,13},{... | collective-permute-start | bytes 28088 | tf_op jit(solution)/shard_map/ppermute | solution.py:16
where the time goes:
time: 299 us; the launch traced here: 298 us
  blocking collectives  122 us (41%)
  starting transfers between devices  57.9 us (19%)
  local copies, waits for them, and re-layouts  48.2 us (16%)
  other arithmetic  46.6 us (16%)
  waiting for transfers between devices  18.1 us (6%)
  between operations  5.17 us (2%)
    psum x3, blocking collectives, statistics(): lax.psum((squares, jnp.sum(own_induced)), ('gx', 'gy', 'gz'))  122 us
    ppermute x12, starting transfers between devices, padded_2(): before = lax.ppermute(last, axis, up)  42.2 us
    reduce_sum x3, other arithmetic, statistics(): squares = jnp.sum(own_residual * own_residual)  27.5 us
    ppermute x12, waiting for transfers between devices, padded_2(): after = lax.ppermute(initial, axis, down)  16.8 us
    slice x7, local copies, waits for them, and re-layouts, padded_2(): initial = lax.slice_in_dim(array, 0, width, axis=dim)  15.9 us
    ppermute x12, starting transfers between devices, padded_2(): after = lax.ppermute(initial, axis, down)  15.7 us
    slice x9, local copies, waits for them, and re-layouts, padded_2(): last = lax.slice_in_dim(array, length - width, length, axis=dim)  13.5 us
    reduce_sum x2, other arithmetic, statistics(): jnp.sum(own_induced)  9.21 us
  transfers between devices with their start and end apart: 24, of which 7 were waited for; matrix products, arithmetic and copies ran while one was open for 12% of the time, Pallas kernels for 0%

commit v1 on v0

--- a/solution.py
+++ b/solution.py
@@ -52,7 +52,13 @@
 
 def statistics(own_residual, own_induced, cells, charge_terms):
     squares = jnp.sum(own_residual * own_residual)
-    square_sum, charge_sum = lax.psum((squares, jnp.sum(own_induced)), ("gx", "gy", "gz"))
+
+    def tell_the_target(panel, row_axis, axis_id):
+        for to_i in (row_axis, axis_id):
+            panel = lax.psum(panel, to_i)
+        return panel
+
+    square_sum, charge_sum = tell_the_target((squares, jnp.sum(own_induced)), ("gy", "gz"), "gx")
     charge_terms.append(charge_sum / cells)
     return jnp.sqrt(square_sum / cells + 1e-06)
 

time: 299 us -> 246 us (0.82)
  blocking collectives: 122 us -> 68.3 us
    psum x3 -> x6, blocking collectives: 122 us -> 68.3 us  [tell_the_target(): panel = lax.psum(panel, to_i)]
  transfers between devices with their start and end apart: 24 -> 24, of which waited for: 7 -> 8; matrix products, arithmetic and copies ran while one was open for 12% -> 15% of each run, Pallas kernels for 0% -> 0%
where the time goes in v1:
time: 246 us; the launch traced here: 244 us
  blocking collectives  68.3 us (28%)
  starting transfers between devices  57.9 us (24%)
  local copies, waits for them, and re-layouts  48.3 us (20%)
  other arithmetic  46.6 us (19%)
  waiting for transfers between devices  18.3 us (7%)
  between operations  5.03 us (2%)
    psum x6, blocking collectives, tell_the_target(): panel = lax.psum(panel, to_i)  68.3 us
    ppermute x12, starting transfers between devices, padded_2(): before = lax.ppermute(last, axis, up)  42.2 us
    reduce_sum x3, other arithmetic, statistics(): squares = jnp.sum(own_residual * own_residual)  27.5 us
    ppermute x12, waiting for transfers between devices, padded_2(): after = lax.ppermute(initial, axis, down)  17 us
    slice x7, local copies, waits for them, and re-layouts, padded_2(): initial = lax.slice_in_dim(array, 0, width, axis=dim)  15.9 us
    ppermute x12, starting transfers between devices, padded_2(): after = lax.ppermute(initial, axis, down)  15.7 us
    slice x9, local copies, waits for them, and re-layouts, padded_2(): last = lax.slice_in_dim(array, length - width, length, axis=dim)  13.6 us
    reduce_sum x2, other arithmetic, statistics(): jnp.sum(own_induced)  9.17 us
  transfers between devices with their start and end apart: 24, of which 8 were waited for; matrix products, arithmetic and copies ran while one was open for 15% of the time, Pallas kernels for 0%

profile of v1, /device:TPU:0, one launch (start us, length us, event | category | flops | bytes accessed | tf_op | source)
XLA Modules:
  0.0 244.5 jit_solution(13689367467582343824)
XLA Ops:
  0.6 0.9 fusion.102
  1.5 1.3 collective-permute-start
  2.8 5.6 %collective-permute-start.2 = (f32[1,128,128]{2,0,1:T(1,128)S(1)}, f32[1,128,128]{2,0,1:T(1,128)S(1)}, u32[]{:S(2)}, u32[]{:S(2)}) collective-permute-start(f32[1,128,128]{2,0,1:T(1,128)S(1)} %bitcast.12), channel_id=1, source_target_pairs={{0,8},{8,16},{16,24},{1,9},{9,17},{17,25},{2,10},{10,18},{18,26},{... | collective-permute-start | bytes 196616 | tf_op jit(solution)/shard_map/ppermute | solution.py:16
  8.4 0.9 fusion.103
  9.3 1.3 collective-permute-start.1
  10.6 4.7 %collective-permute-start.3 = (f32[1,128,128]{2,0,1:T(1,128)S(1)}, f32[1,128,128]{2,0,1:T(1,128)S(1)}, u32[]{:S(2)}, u32[]{:S(2)}) collective-permute-start(f32[1,128,128]{2,0,1:T(1,128)S(1)} %bitcast.10), channel_id=1, source_target_pairs={{0,8},{8,16},{16,24},{1,9},{9,17},{17,25},{2,10},{10,18},{18,26},{... | collective-permute-start | bytes 196616 | tf_op jit(solution)/shard_map/ppermute | solution.py:16
  15.3 4.7 %fusion.88 = (f32[]{:T(128)}, f32[16,128,128]{2,0,1:T(8,128)}, f32[16,128,128]{2,0,1:T(8,128)S(1)}) fusion(f32[16,128,128]{2,1,0:T(8,128)} %param.4, f32[16,128,128]{2,1,0:T(8,128)} %param.6), kind=kLoop, calls=%fused_computation.203 | loop fusion | flops 3145727 | bytes 4194308 | tf_op jit(solution)/shard_map/reduce_sum | solution.py:61
  20.7 1.3 collective-permute-start.4
  22.0 4.5 %collective-permute-start.6 = (f32[18,1,128]{2,0,1:T(8,128)S(1)}, f32[18,1,128]{2,0,1:T(8,128)S(1)}, u32[]{:S(2)}, u32[]{:S(2)}) collective-permute-start(f32[18,1,128]{2,0,1:T(8,128)S(1)} %get-tuple-element.48), channel_id=1, source_target_pairs={{0,4},{1,5},{2,6},{3,7},{8,12},{9,13},{10,14},{11,15},{16,20},{17,... | collective-permute-start | bytes 27656 | tf_op jit(solution)/shard_map/ppermute | solution.py:16
  26.6 1.3 collective-permute-start.7
  27.9 1.3 collective-permute-start.5
  29.5 2.2 fusion.98
  31.6 2.4 copy.168
  34.0 2.4 copy.162
  36.4 1.3 collective-permute-start.8
  37.7 3.0 %collective-permute-start.10 = (f32[18,130,1]{1,0,2:T(8,128)S(1)}, f32[18,130,1]{1,0,2:T(8,128)S(1)}, u32[]{:S(2)}, u32[]{:S(2)}) collective-permute-start(f32[18,130,1]{1,0,2:T(8,128)S(1)} %copy.168), channel_id=1, source_target_pairs={{0,1},{1,2},{2,3},{4,5},{5,6},{6,7},{8,9},{9,10},{10,11},{12,13},{... | collective-permute-start | bytes 28088 | tf_op jit(solution)/shard_map/ppermute | solution.py:16
  41.0 2.2 fusion.99
  43.1 2.4 copy.165
  45.5 1.3 collective-permute-start.9
  46.8 2.4 copy.171
  49.2 4.1 %collective-permute-start.11 = (f32[18,130,1]{1,0,2:T(8,128)S(1)}, f32[18,130,1]{1,0,2:T(8,128)S(1)}, u32[]{:S(2)}, u32[]{:S(2)}) collective-permute-start(f32[18,130,1]{1,0,2:T(8,128)S(1)} %copy.171), channel_id=1, source_target_pairs={{0,1},{1,2},{2,3},{4,5},{5,6},{6,7},{8,9},{9,10},{10,11},{12,13},{... | collective-permute-start | bytes 28088 | tf_op jit(solution)/shard_map/ppermute | solution.py:16
  53.3 2.1 copy.169
  55.4 2.1 copy.163
  57.5 2.1 copy.166
  59.6 2.1 copy.172
  61.8 9.7 %multiply_reduce_fusion.2 = (f32[]{:T(128)}, f32[16,128,128]{2,0,1:T(8,128)}, f32[16,128,128]{2,0,1:T(8,128)}, f32[16,128,128]{2,0,1:T(8,128)}) fusion(f32[16,128,128]{2,0,1:T(8,128)} %get-tuple-element.23, f32[16,128,128]{2,0,1:T(8,128)S(1)} %get-tuple-element.59, f32[18,1,128]{2,0,1:T(8,128)S(1)} %collective-permute-done.5, ...), kind=kLoop, calls=%fused_computation.183 | loop fusion | flops 23068672 | bytes 7676484 | tf_op jit(solution)/shard_map/reduce_sum | solution.py:54
  71.5 14.7 %psum.84 = f32[]{:T(128)} all-reduce(f32[]{:T(128)} %get-tuple-element.31), channel_id=1, replica_groups=mesh['gx'=4,'gy'=2,'gz'=4] {'gy','gz'}, use_global_device_ids=true, to_apply=%region_1.2 | all-reduce | flops 1 | bytes 8 | tf_op jit(solution)/shard_map/psum | solution.py:58
  86.1 10.7 %psum.85 = f32[]{:T(128)} all-reduce(f32[]{:T(128)} %psum.84), channel_id=1, replica_groups=mesh['gx'=4,'gy'=2,'gz'=4] {'gx'}, use_global_device_ids=true, to_apply=%region_2.3 | all-reduce | flops 1 | bytes 8 | tf_op jit(solution)/shard_map/psum | solution.py:58
  97.6 5.9 %fusion.16 = (f32[16,128,128]{2,0,1:T(8,128)S(1)}, f32[16,128,128]{2,0,1:T(8,128)}) fusion(f32[16,128,128]{2,0,1:T(8,128)} %get-tuple-element.32, f32[16,128,128]{2,1,0:T(8,128)S(1)} %copy-done, f32[]{:T(128)S(6)} %div.73, f32[16,128,128]{2,1,0:T(8,128)} %param.4, f32[16,128,128]{2,0,1:T(8,128)} %get-tuple-element.34, f32[16,128,128]{2,0,1:T(8,128)} %get-tuple-element.33, ...), kind=kLoop, calls=%fused_computation.32 | loop fusion | flops 11534336 | bytes 8538116 | tf_op jit(solution)/shard_map/add | solution.py:85
  103.6 2.5 %collective-permute-start.13 = (f32[1,128,128]{2,0,1:T(1,128)S(1)}, f32[1,128,128]{2,0,1:T(1,128)S(1)}, u32[]{:S(2)}, u32[]{:S(2)}) collective-permute-start(f32[1,128,128]{2,0,1:T(1,128)S(1)} %get-tuple-element.53), channel_id=1, source_target_pairs={{0,8},{8,16},{16,24},{1,9},{9,17},{17,25},{2,10},{10,18},{18,26},{... | collective-permute-start | bytes 196616 | tf_op jit(solution)/shard_map/ppermute | solution.py:16
  106.1 1.3 collective-permute-start.12
  108.0 4.3 %collective-permute-done.12 = f32[1,128,128]{2,0,1:T(1,128)S(1)} collective-permute-done((f32[1,128,128]{2,0,1:T(1,128)S(1)}, f32[1,128,128]{2,0,1:T(1,128)S(1)}, u32[]{:S(2)}, u32[]{:S(2)}) %collective-permute-start.12) | collective-permute-done | bytes 65568 | tf_op jit(solution)/shard_map/ppermute | solution.py:17
  112.3 4.0 %collective-permute-start.15 = (f32[18,1,128]{2,0,1:T(8,128)S(1)}, f32[18,1,128]{2,0,1:T(8,128)S(1)}, u32[]{:S(2)}, u32[]{:S(2)}) collective-permute-start(f32[18,1,128]{2,0,1:T(8,128)S(1)} %get-tuple-element.45), channel_id=1, source_target_pairs={{0,4},{1,5},{2,6},{3,7},{8,12},{9,13},{10,14},{11,15},{16,20},{17,... | collective-permute-start | bytes 27656 | tf_op jit(solution)/shard_map/ppermute | solution.py:16
  116.3 1.3 collective-permute-start.14
  117.7 4.2 %collective-permute-done.14 = f32[18,1,128]{2,0,1:T(8,128)S(1)} collective-permute-done((f32[18,1,128]{2,0,1:T(8,128)S(1)}, f32[18,1,128]{2,0,1:T(8,128)S(1)}, u32[]{:S(2)}, u32[]{:S(2)}) %collective-permute-start.14) | collective-permute-done | bytes 9248 | tf_op jit(solution)/shard_map/ppermute | solution.py:17
  122.1 2.2 fusion.97
  124.3 2.4 copy.182
  126.7 1.3 collective-permute-start.16
  128.0 2.4 copy.184
  130.3 3.0 %collective-permute-start.17 = (f32[18,130,1]{1,0,2:T(8,128)S(1)}, f32[18,130,1]{1,0,2:T(8,128)S(1)}, u32[]{:S(2)}, u32[]{:S(2)}) collective-permute-start(f32[18,130,1]{1,0,2:T(8,128)S(1)} %copy.184), channel_id=1, source_target_pairs={{0,1},{1,2},{2,3},{4,5},{5,6},{6,7},{8,9},{9,10},{10,11},{12,13},{... | collective-permute-start | bytes 28088 | tf_op jit(solution)/shard_map/ppermute | solution.py:16
  133.4 2.1 copy.183
  135.5 2.1 copy.185
  137.6 8.9 %multiply_reduce_fusion.1 = (f32[]{:T(128)}, f32[16,128,128]{2,0,1:T(8,128)}) fusion(f32[16,128,128]{2,0,1:T(8,128)S(1)} %get-tuple-element.29, f32[16,128,128]{2,1,0:T(8,128)S(1)} %copy-done, f32[16,128,128]{2,0,1:T(8,128)} %get-tuple-element.34, f32[18,1,128]{2,0,1:T(8,128)S(1)} %collective-permute-done.14, ...), kind=kLoop, calls=%fused_computation.178 | loop fusion | flops 20709376 | bytes 7657764 | tf_op jit(solution)/shard_map/reduce_sum | solution.py:54
  146.4 12.4 %psum.86 = f32[]{:T(128)} all-reduce(f32[]{:T(128)} %get-tuple-element.27), channel_id=1, replica_groups=mesh['gx'=4,'gy'=2,'gz'=4] {'gy','gz'}, use_global_device_ids=true, to_apply=%region_4.5 | all-reduce | flops 1 | bytes 8 | tf_op jit(solution)/shard_map/psum | solution.py:58
  158.9 9.0 %psum.87 = f32[]{:T(128)} all-reduce(f32[]{:T(128)} %psum.86), channel_id=1, replica_groups=mesh['gx'=4,'gy'=2,'gz'=4] {'gx'}, use_global_device_ids=true, to_apply=%region_5.6 | all-reduce | flops 1 | bytes 8 | tf_op jit(solution)/shard_map/psum | solution.py:58
  168.6 4.4 %fusion.87 = (f32[]{:T(128)}, f32[]{:T(128)}, f32[16,128,128]{2,0,1:T(8,128)S(1)}) fusion(f32[16,128,128]{2,0,1:T(8,128)S(1)} %get-tuple-element.29, f32[16,128,128]{2,1,0:T(8,128)S(1)} %copy-done, f32[16,128,128]{2,0,1:T(8,128)} %get-tuple-element.30, f32[16,128,128]{2,0,1:T(8,128)} %get-tuple-element.28, f32[]{:T(128)S(6)} %div.76), kind=kLoop, calls=%fused_computation.202 | loop fusion | flops 8388606 | bytes 5242892 | tf_op jit(solution)/shard_map/reduce_sum | solution.py:61
  173.1 3.9 %collective-permute-start.19 = (f32[1,128,128]{2,0,1:T(1,128)S(1)}, f32[1,128,128]{2,0,1:T(1,128)S(1)}, u32[]{:S(2)}, u32[]{:S(2)}) collective-permute-start(f32[1,128,128]{2,0,1:T(1,128)S(1)} %get-tuple-element.51), channel_id=1, source_target_pairs={{0,8},{8,16},{16,24},{1,9},{9,17},{17,25},{2,10},{10,18},{18,26},{... | collective-permute-start | bytes 196616 | tf_op jit(solution)/shard_map/ppermute | solution.py:16
  177.0 1.3 collective-permute-start.18
  178.9 4.3 %collective-permute-done.18 = f32[1,128,128]{2,0,1:T(1,128)S(1)} collective-permute-done((f32[1,128,128]{2,0,1:T(1,128)S(1)}, f32[1,128,128]{2,0,1:T(1,128)S(1)}, u32[]{:S(2)}, u32[]{:S(2)}) %collective-permute-start.18) | collective-permute-done | bytes 65568 | tf_op jit(solution)/shard_map/ppermute | solution.py:17
  183.2 2.3 collective-permute-start.21
  185.5 1.3 collective-permute-start.20
  186.9 4.2 %collective-permute-done.20 = f32[18,1,128]{2,0,1:T(8,128)S(1)} collective-permute-done((f32[18,1,128]{2,0,1:T(8,128)S(1)}, f32[18,1,128]{2,0,1:T(8,128)S(1)}, u32[]{:S(2)}, u32[]{:S(2)}) %collective-permute-start.20) | collective-permute-done | bytes 9248 | tf_op jit(solution)/shard_map/ppermute | solution.py:17
  191.4 2.2 fusion.96
  193.5 2.4 copy.189
  195.9 1.5 collective-permute-start.22
  197.4 2.4 copy.191
  199.8 3.2 %collective-permute-start.23 = (f32[18,130,1]{1,0,2:T(8,128)S(1)}, f32[18,130,1]{1,0,2:T(8,128)S(1)}, u32[]{:S(2)}, u32[]{:S(2)}) collective-permute-start(f32[18,130,1]{1,0,2:T(8,128)S(1)} %copy.191), channel_id=1, source_target_pairs={{0,1},{1,2},{2,3},{4,5},{5,6},{6,7},{8,9},{9,10},{10,11},{12,13},{... | collective-permute-start | bytes 28088 | tf_op jit(solution)/shard_map/ppermute | solution.py:16
  203.0 2.1 copy.190
  205.1 2.1 copy.192
  207.2 8.9 %multiply_reduce_fusion = (f32[]{:T(128)}, f32[16,128,128]{2,0,1:T(8,128)}) fusion(f32[16,128,128]{2,0,1:T(8,128)S(1)} %copy-done.2, f32[16,128,128]{2,1,0:T(8,128)S(1)} %copy-done, f32[16,128,128]{2,0,1:T(8,128)} %get-tuple-element.34, f32[18,1,128]{2,0,1:T(8,128)S(1)} %collective-permute-done.20, f32[1,128,128]{2,0,1:T(1,128)S(1)} %collective-permute-done.18, ...), kind=kLoop, calls=%fused_computation.174 | loop fusion | flops 20709376 | bytes 7657764 | tf_op jit(solution)/shard_map/reduce_sum | solution.py:54
  216.1 12.5 %all-reduce = (f32[]{:T(128)}, f32[]{:T(128)}, f32[]{:T(128)}, f32[]{:T(128)}) all-reduce(f32[]{:T(128)} %get-tuple-element.25, f32[]{:T(128)} %get-tuple-element.13, f32[]{:T(128)} %get-tuple-element.12, f32[]{:T(128)} %get-tuple-element.22), channel_id=1, replica_groups=mesh['gx'=4,'gy'=2,'gz'=4] {'gy','gz'}, use_global_device_ids=true, to_apply=%region_7.8 | all-reduce | flops 4 | bytes 32 | tf_op jit(solution)/shard_map/psum | solution.py:58
  228.6 9.0 %all-reduce.1 = (f32[]{:T(128)}, f32[]{:T(128)}, f32[]{:T(128)}, f32[]{:T(128)}) all-reduce(f32[]{:T(128)} %get-tuple-element.14, f32[]{:T(128)} %get-tuple-element.15, f32[]{:T(128)} %get-tuple-element.16, f32[]{:T(128)} %get-tuple-element.17), channel_id=1, replica_groups=mesh['gx'=4,'gy'=2,'gz'=4] {'gx'}, use_global_device_ids=true, to_apply=%region_8.9 | all-reduce | flops 4 | bytes 32 | tf_op jit(solution)/shard_map/psum | solution.py:58
  240.1 2.5 %fusion.20 = f32[16,128,128]{2,0,1:T(8,128)S(1)} fusion(f32[16,128,128]{2,0,1:T(8,128)S(1)} %copy-done.2, f32[16,128,128]{2,0,1:T(8,128)} %get-tuple-element.30, f32[16,128,128]{2,0,1:T(8,128)} %get-tuple-element.26, f32[16,128,128]{2,1,0:T(8,128)S(1)} %copy-done, f32[]{:T(128)S(6)} %div.79), kind=kLoop, calls=%fused_computation.36 | loop fusion | flops 2621440 | bytes 5242884 | tf_op jit(solution)/shard_map/add | solution.py:85
  242.6 1.3 copy.196
  (40 shorter events, 3.8 us)
Async XLA Ops:
  1.5 19.1 %collective-permute-start = (f32[1,128,128]{2,0,1:T(1,128)S(1)}, f32[1,128,128]{2,0,1:T(1,128)S(1)}, u32[]{:S(2)}, u32[]{:S(2)}) collective-permute-start(f32[1,128,128]{2,0,1:T(1,128)S(1)} %bitcast.13), channel_id=1, source_target_pairs={{8,0},{16,8},{24,16},{9,1},{17,9},{25,17},{10,2},{18,10},{26,18},{... | collective-permute-start | bytes 196616 | tf_op jit(solution)/shard_map/ppermute | solution.py:17
  2.8 17.9 %collective-permute-start.2 = (f32[1,128,128]{2,0,1:T(1,128)S(1)}, f32[1,128,128]{2,0,1:T(1,128)S(1)}, u32[]{:S(2)}, u32[]{:S(2)}) collective-permute-start(f32[1,128,128]{2,0,1:T(1,128)S(1)} %bitcast.12), channel_id=1, source_target_pairs={{0,8},{8,16},{16,24},{1,9},{9,17},{17,25},{2,10},{10,18},{18,26},{... | collective-permute-start | bytes 196616 | tf_op jit(solution)/shard_map/ppermute | solution.py:16
  9.3 17.3 %collective-permute-start.1 = (f32[1,128,128]{2,0,1:T(1,128)S(1)}, f32[1,128,128]{2,0,1:T(1,128)S(1)}, u32[]{:S(2)}, u32[]{:S(2)}) collective-permute-start(f32[1,128,128]{2,0,1:T(1,128)S(1)} %bitcast.11), channel_id=1, source_target_pairs={{8,0},{16,8},{24,16},{9,1},{17,9},{25,17},{10,2},{18,10},{26,18},{... | collective-permute-start | bytes 196616 | tf_op jit(solution)/shard_map/ppermute | solution.py:17
  10.6 9.4 %copy-start.3 = (f32[16,128,128]{2,1,0:T(8,128)S(1)}, f32[16,128,128]{2,1,0:T(8,128)}, u32[]{:S(2)}) copy-start(f32[16,128,128]{2,1,0:T(8,128)} %param.5) | copy-start | bytes 3145732
  10.6 16.0 %collective-permute-start.3 = (f32[1,128,128]{2,0,1:T(1,128)S(1)}, f32[1,128,128]{2,0,1:T(1,128)S(1)}, u32[]{:S(2)}, u32[]{:S(2)}) collective-permute-start(f32[1,128,128]{2,0,1:T(1,128)S(1)} %bitcast.10), channel_id=1, source_target_pairs={{0,8},{8,16},{16,24},{1,9},{9,17},{17,25},{2,10},{10,18},{18,26},{... | collective-permute-start | bytes 196616 | tf_op jit(solution)/shard_map/ppermute | solution.py:16
  20.7 8.5 %collective-permute-start.4 = (f32[18,1,128]{2,0,1:T(8,128)S(1)}, f32[18,1,128]{2,0,1:T(8,128)S(1)}, u32[]{:S(2)}, u32[]{:S(2)}) collective-permute-start(f32[18,1,128]{2,0,1:T(8,128)S(1)} %get-tuple-element.47), channel_id=1, source_target_pairs={{4,0},{5,1},{6,2},{7,3},{12,8},{13,9},{14,10},{15,11},{20,16},{21,... | collective-permute-start | bytes 27656 | tf_op jit(solution)/shard_map/ppermute | solution.py:17
  22.0 7.2 %collective-permute-start.6 = (f32[18,1,128]{2,0,1:T(8,128)S(1)}, f32[18,1,128]{2,0,1:T(8,128)S(1)}, u32[]{:S(2)}, u32[]{:S(2)}) collective-permute-start(f32[18,1,128]{2,0,1:T(8,128)S(1)} %get-tuple-element.48), channel_id=1, source_target_pairs={{0,4},{1,5},{2,6},{3,7},{8,12},{9,13},{10,14},{11,15},{16,20},{17,... | collective-permute-start | bytes 27656 | tf_op jit(solution)/shard_map/ppermute | solution.py:16
  26.6 14.1 %collective-permute-start.7 = (f32[18,1,128]{2,0,1:T(8,128)S(1)}, f32[18,1,128]{2,0,1:T(8,128)S(1)}, u32[]{:S(2)}, u32[]{:S(2)}) collective-permute-start(f32[18,1,128]{2,0,1:T(8,128)S(1)} %get-tuple-element.49), channel_id=1, source_target_pairs={{0,4},{1,5},{2,6},{3,7},{8,12},{9,13},{10,14},{11,15},{16,20},{17,... | collective-permute-start | bytes 27656 | tf_op jit(solution)/shard_map/ppermute | solution.py:16
  27.9 12.8 %collective-permute-start.5 = (f32[18,1,128]{2,0,1:T(8,128)S(1)}, f32[18,1,128]{2,0,1:T(8,128)S(1)}, u32[]{:S(2)}, u32[]{:S(2)}) collective-permute-start(f32[18,1,128]{2,0,1:T(8,128)S(1)} %get-tuple-element.50), channel_id=1, source_target_pairs={{4,0},{5,1},{6,2},{7,3},{12,8},{13,9},{14,10},{15,11},{20,16},{21,... | collective-permute-start | bytes 27656 | tf_op jit(solution)/shard_map/ppermute | solution.py:17
  36.4 19.1 %collective-permute-start.8 = (f32[18,130,1]{1,0,2:T(8,128)S(1)}, f32[18,130,1]{1,0,2:T(8,128)S(1)}, u32[]{:S(2)}, u32[]{:S(2)}) collective-permute-start(f32[18,130,1]{1,0,2:T(8,128)S(1)} %copy.162), channel_id=1, source_target_pairs={{1,0},{2,1},{3,2},{5,4},{6,5},{7,6},{9,8},{10,9},{11,10},{13,12},{... | collective-permute-start | bytes 28088 | tf_op jit(solution)/shard_map/ppermute | solution.py:17
  37.7 15.6 %collective-permute-start.10 = (f32[18,130,1]{1,0,2:T(8,128)S(1)}, f32[18,130,1]{1,0,2:T(8,128)S(1)}, u32[]{:S(2)}, u32[]{:S(2)}) collective-permute-start(f32[18,130,1]{1,0,2:T(8,128)S(1)} %copy.168), channel_id=1, source_target_pairs={{0,1},{1,2},{2,3},{4,5},{5,6},{6,7},{8,9},{9,10},{10,11},{12,13},{... | collective-permute-start | bytes 28088 | tf_op jit(solution)/shard_map/ppermute | solution.py:16
  45.5 12.1 %collective-permute-start.9 = (f32[18,130,1]{1,0,2:T(8,128)S(1)}, f32[18,130,1]{1,0,2:T(8,128)S(1)}, u32[]{:S(2)}, u32[]{:S(2)}) collective-permute-start(f32[18,130,1]{1,0,2:T(8,128)S(1)} %copy.165), channel_id=1, source_target_pairs={{1,0},{2,1},{3,2},{5,4},{6,5},{7,6},{9,8},{10,9},{11,10},{13,12},{... | collective-permute-start | bytes 28088 | tf_op jit(solution)/shard_map/ppermute | solution.py:17
  49.2 10.5 %collective-permute-start.11 = (f32[18,130,1]{1,0,2:T(8,128)S(1)}, f32[18,130,1]{1,0,2:T(8,128)S(1)}, u32[]{:S(2)}, u32[]{:S(2)}) collective-permute-start(f32[18,130,1]{1,0,2:T(8,128)S(1)} %copy.171), channel_id=1, source_target_pairs={{0,1},{1,2},{2,3},{4,5},{5,6},{6,7},{8,9},{9,10},{10,11},{12,13},{... | collective-permute-start | bytes 28088 | tf_op jit(solution)/shard_map/ppermute | solution.py:16
  61.8 35.8 %copy-start = (f32[16,128,128]{2,1,0:T(8,128)S(1)}, f32[16,128,128]{2,1,0:T(8,128)}, u32[]{:S(2)}) copy-start(f32[16,128,128]{2,1,0:T(8,128)} %param.6) | copy-start | bytes 3145732
  103.6 4.4 %collective-permute-start.13 = (f32[1,128,128]{2,0,1:T(1,128)S(1)}, f32[1,128,128]{2,0,1:T(1,128)S(1)}, u32[]{:S(2)}, u32[]{:S(2)}) collective-permute-start(f32[1,128,128]{2,0,1:T(1,128)S(1)} %get-tuple-element.53), channel_id=1, source_target_pairs={{0,8},{8,16},{16,24},{1,9},{9,17},{17,25},{2,10},{10,18},{18,26},{... | collective-permute-start | bytes 196616 | tf_op jit(solution)/shard_map/ppermute | solution.py:16
  106.1 6.2 %collective-permute-start.12 = (f32[1,128,128]{2,0,1:T(1,128)S(1)}, f32[1,128,128]{2,0,1:T(1,128)S(1)}, u32[]{:S(2)}, u32[]{:S(2)}) collective-permute-start(f32[1,128,128]{2,0,1:T(1,128)S(1)} %get-tuple-element.54), channel_id=1, source_target_pairs={{8,0},{16,8},{24,16},{9,1},{17,9},{25,17},{10,2},{18,10},{26,18},{... | collective-permute-start | bytes 196616 | tf_op jit(solution)/shard_map/ppermute | solution.py:17
  112.3 5.4 %collective-permute-start.15 = (f32[18,1,128]{2,0,1:T(8,128)S(1)}, f32[18,1,128]{2,0,1:T(8,128)S(1)}, u32[]{:S(2)}, u32[]{:S(2)}) collective-permute-start(f32[18,1,128]{2,0,1:T(8,128)S(1)} %get-tuple-element.45), channel_id=1, source_target_pairs={{0,4},{1,5},{2,6},{3,7},{8,12},{9,13},{10,14},{11,15},{16,20},{17,... | collective-permute-start | bytes 27656 | tf_op jit(solution)/shard_map/ppermute | solution.py:16
  116.3 5.6 %collective-permute-start.14 = (f32[18,1,128]{2,0,1:T(8,128)S(1)}, f32[18,1,128]{2,0,1:T(8,128)S(1)}, u32[]{:S(2)}, u32[]{:S(2)}) collective-permute-start(f32[18,1,128]{2,0,1:T(8,128)S(1)} %get-tuple-element.46), channel_id=1, source_target_pairs={{4,0},{5,1},{6,2},{7,3},{12,8},{13,9},{14,10},{15,11},{20,16},{21,... | collective-permute-start | bytes 27656 | tf_op jit(solution)/shard_map/ppermute | solution.py:17
  126.7 6.7 %collective-permute-start.16 = (f32[18,130,1]{1,0,2:T(8,128)S(1)}, f32[18,130,1]{1,0,2:T(8,128)S(1)}, u32[]{:S(2)}, u32[]{:S(2)}) collective-permute-start(f32[18,130,1]{1,0,2:T(8,128)S(1)} %copy.182), channel_id=1, source_target_pairs={{1,0},{2,1},{3,2},{5,4},{6,5},{7,6},{9,8},{10,9},{11,10},{13,12},{... | collective-permute-start | bytes 28088 | tf_op jit(solution)/shard_map/ppermute | solution.py:17
  130.3 5.1 %collective-permute-start.17 = (f32[18,130,1]{1,0,2:T(8,128)S(1)}, f32[18,130,1]{1,0,2:T(8,128)S(1)}, u32[]{:S(2)}, u32[]{:S(2)}) collective-permute-start(f32[18,130,1]{1,0,2:T(8,128)S(1)} %copy.184), channel_id=1, source_target_pairs={{0,1},{1,2},{2,3},{4,5},{5,6},{6,7},{8,9},{9,10},{10,11},{12,13},{... | collective-permute-start | bytes 28088 | tf_op jit(solution)/shard_map/ppermute | solution.py:16
  173.0 18.1 %copy-start.1 = (f32[16,128,128]{2,0,1:T(8,128)}, f32[16,128,128]{2,0,1:T(8,128)S(1)}, u32[]{:S(2)}) copy-start(f32[16,128,128]{2,0,1:T(8,128)S(1)} %get-tuple-element.24) | copy-start | bytes 3145732
  173.1 5.8 %collective-permute-start.19 = (f32[1,128,128]{2,0,1:T(1,128)S(1)}, f32[1,128,128]{2,0,1:T(1,128)S(1)}, u32[]{:S(2)}, u32[]{:S(2)}) collective-permute-start(f32[1,128,128]{2,0,1:T(1,128)S(1)} %get-tuple-element.51), channel_id=1, source_target_pairs={{0,8},{8,16},{16,24},{1,9},{9,17},{17,25},{2,10},{10,18},{18,26},{... | collective-permute-start | bytes 196616 | tf_op jit(solution)/shard_map/ppermute | solution.py:16
  177.0 6.2 %collective-permute-start.18 = (f32[1,128,128]{2,0,1:T(1,128)S(1)}, f32[1,128,128]{2,0,1:T(1,128)S(1)}, u32[]{:S(2)}, u32[]{:S(2)}) collective-permute-start(f32[1,128,128]{2,0,1:T(1,128)S(1)} %get-tuple-element.52), channel_id=1, source_target_pairs={{8,0},{16,8},{24,16},{9,1},{17,9},{25,17},{10,2},{18,10},{26,18},{... | collective-permute-start | bytes 196616 | tf_op jit(solution)/shard_map/ppermute | solution.py:17
  183.2 3.7 %collective-permute-start.21 = (f32[18,1,128]{2,0,1:T(8,128)S(1)}, f32[18,1,128]{2,0,1:T(8,128)S(1)}, u32[]{:S(2)}, u32[]{:S(2)}) collective-permute-start(f32[18,1,128]{2,0,1:T(8,128)S(1)} %get-tuple-element.43), channel_id=1, source_target_pairs={{0,4},{1,5},{2,6},{3,7},{8,12},{9,13},{10,14},{11,15},{16,20},{17,... | collective-permute-start | bytes 27656 | tf_op jit(solution)/shard_map/ppermute | solution.py:16
  185.5 5.6 %collective-permute-start.20 = (f32[18,1,128]{2,0,1:T(8,128)S(1)}, f32[18,1,128]{2,0,1:T(8,128)S(1)}, u32[]{:S(2)}, u32[]{:S(2)}) collective-permute-start(f32[18,1,128]{2,0,1:T(8,128)S(1)} %get-tuple-element.44), channel_id=1, source_target_pairs={{4,0},{5,1},{6,2},{7,3},{12,8},{13,9},{14,10},{15,11},{20,16},{21,... | collective-permute-start | bytes 27656 | tf_op jit(solution)/shard_map/ppermute | solution.py:17
  195.9 7.1 %collective-permute-start.22 = (f32[18,130,1]{1,0,2:T(8,128)S(1)}, f32[18,130,1]{1,0,2:T(8,128)S(1)}, u32[]{:S(2)}, u32[]{:S(2)}) collective-permute-start(f32[18,130,1]{1,0,2:T(8,128)S(1)} %copy.189), channel_id=1, source_target_pairs={{1,0},{2,1},{3,2},{5,4},{6,5},{7,6},{9,8},{10,9},{11,10},{13,12},{... | collective-permute-start | bytes 28088 | tf_op jit(solution)/shard_map/ppermute | solution.py:17
  199.8 7.4 %copy-start.2 = (f32[16,128,128]{2,0,1:T(8,128)S(1)}, f32[16,128,128]{2,0,1:T(8,128)}, u32[]{:S(2)}) copy-start(f32[16,128,128]{2,0,1:T(8,128)} %copy-done.1) | copy-start | bytes 3145732
  199.8 5.3 %collective-permute-start.23 = (f32[18,130,1]{1,0,2:T(8,128)S(1)}, f32[18,130,1]{1,0,2:T(8,128)S(1)}, u32[]{:S(2)}, u32[]{:S(2)}) collective-permute-start(f32[18,130,1]{1,0,2:T(8,128)S(1)} %copy.191), channel_id=1, source_target_pairs={{0,1},{1,2},{2,3},{4,5},{5,6},{6,7},{8,9},{9,10},{10,11},{12,13},{... | collective-permute-start | bytes 28088 | tf_op jit(solution)/shard_map/ppermute | solution.py:16
